TPU v7x, 256 devices: a whole 4x4x8 slice. The times are simulated.
256 devices in a mesh: ops: 64 (over x, z, core), sec: 4 (over y).
Axes of the slice: x: 4, y: 4, z: 8, core: 2. Of those that a mesh axis runs over, the one named last changes fastest.
Arguments:
- operators: bfloat16 [128, 8, 768, 768], P('ops', 'sec'), may hold values from -6 to 6
- basis: bfloat16 [8, 768, 768], P('sec'), may hold values from -0.21875 to 0.21875
- shift: int32 [128], replicated, may hold values from -1 to 1
- dest: int32 [128], replicated, may hold values from 0 to 127, each once
- sector_sizes: int32 [8], replicated, may hold values from 384 to 768
Outputs:
- renormalized: bfloat16 [128, 8, 768, 768], P('ops', 'sec')
Inputs may be any that keep to these rules, and one draw needn't show every extreme that they name: `shift`: each pair's offset is -1, 0 or 1. dest names every index of 0 to 127 once.
All inputs are finite; a program needn't handle non-finite values.
Results may differ from a plain program's by a relative error of at most 0.0049.
Values may be sent and summed in bfloat16 or wider, within the bound.
No kernel may reach another device: no remote copies, remote signals or barrier semaphores. Data moves between devices by JAX's collectives and lax.ppermute only.
A program may use at most 128 MiB of HBM per device.

v0:
```python
import jax
import jax.numpy as jnp
from jax import lax
from jax.sharding import PartitionSpec as P


def with_halo(block, sides, width):
    for axis, dim in sides:
        count = lax.axis_size(axis)
        forward = [(i, i + 1) for i in range(count - 1)]
        forward.append((count - 1, 0))
        backward = [(target, source) for source, target in forward]
        low = lax.ppermute(
            lax.slice_in_dim(block, block.shape[dim] - width, None, axis=dim), axis, forward
        )
        high = lax.ppermute(lax.slice_in_dim(block, 0, width, axis=dim), axis, backward)
        block = jnp.concatenate([low, block, high], axis=dim)
    return block


def body(operators, basis, shift, dest, sector_sizes):
    pair_dev = operators.shape[0]
    sector_dev = operators.shape[1]
    width = operators.shape[3]
    ops_count = lax.axis_size("ops")
    total_sectors = sector_dev * lax.axis_size("sec")
    sector_pos = lax.axis_index("sec")
    ops_pos = lax.axis_index("ops")
    nearby = with_halo(basis, (("sec", 0),), 1)
    near_ids = (
        sector_pos * sector_dev - 1 + jnp.arange(sector_dev + 2, dtype=jnp.int32)
    ) % total_sectors
    own_local = jnp.arange(sector_dev, dtype=jnp.int32) + 1
    columns = jnp.arange(width, dtype=jnp.int32)
    near_sizes = jnp.take(sector_sizes, near_ids)
    kept = columns[None, :] < near_sizes[:, None]
    kept_near = jnp.where(kept[:, None, :], nearby, jnp.zeros_like(nearby))
    own_basis = jnp.take(kept_near, own_local, axis=0)
    source = jnp.argsort(dest, stable=True)
    mine = lax.dynamic_slice_in_dim(source, ops_pos * pair_dev, pair_dev)
    offsets = jnp.take(shift, mine)
    strip = width // ops_count
    split = operators.reshape(pair_dev, sector_dev, ops_count, strip, width)
    spread = lax.all_to_all(split, "ops", split_axis=2, concat_axis=0, tiled=True)
    ordered = jnp.take(spread, source, axis=0)
    returned = lax.all_to_all(ordered, "ops", split_axis=0, concat_axis=2, tiled=True)
    blocks = returned.reshape(pair_dev, sector_dev, width, width)
    target_local = own_local[None, :] + offsets[:, None]
    half = jnp.einsum(
        "psab,sbc->psac", blocks, own_basis, preferred_element_type=jnp.float32
    ).astype(jnp.bfloat16)
    targets = jnp.take(kept_near, target_local.reshape(-1), axis=0)
    targets = targets.reshape(blocks.shape[0], sector_dev, width, width)
    return jnp.einsum("psba,psbc->psac", targets, half, preferred_element_type=jnp.float32).astype(
        jnp.bfloat16
    )


def solution(mesh):
    return jax.shard_map(
        body,
        mesh=mesh,
        in_specs=(P("ops", "sec", None, None), P("sec", None, None), P(), P(), P()),
        out_specs=P("ops", "sec", None, None),
        check_vma=False,
    )
```

profile of v0, /device:TPU:1, one launch (start us, length us, event | category | flops | bytes accessed | tf_op | source)
XLA Modules:
  0.0 295.1 jit_solution(11162149202697768702)
XLA Ops:
  0.0 9.4 %copy.12 = bf16[2,2,768,768]{3,1,2,0:T(2,128)(2,1)} copy(bf16[2,2,768,768]{3,2,1,0:T(8,128)(2,1)} %param.5) | data formatting | bytes 9437184 | tf_op args[0]
  9.4 7.7 %copy.13 = bf16[2,2,64,12,768]{4,1,3,0,2:T(2,128)(2,1)} copy(bf16[2,2,64,12,768]{4,1,3,2,0:T(2,128)(2,1)} %bitcast.33) | data formatting | bytes 9437184 | tf_op jit(solution)/shard_map/reshape | solution.py:43
  17.1 13.3 %all-to-all-start = ((bf16[2,2,64,12,768]{4,1,3,0,2:T(2,128)(2,1)}), bf16[2,2,64,12,768]{4,1,3,0,2:T(2,128)(2,1)}, u32[]{:S(2)}, u32[]{:S(2)}) async-start(bf16[2,2,64,12,768]{4,1,3,0,2:T(2,128)(2,1)} %copy.13), calls=%async_computation | async-start | bytes 9437184 | tf_op jit(solution)/shard_map/all_to_all | solution.py:44
  30.5 2.5 sort.17
  33.0 104.5 %all-to-all-done = bf16[2,2,64,12,768]{4,1,3,0,2:T(2,128)(2,1)} async-done(((bf16[2,2,64,12,768]{4,1,3,0,2:T(2,128)(2,1)}), bf16[2,2,64,12,768]{4,1,3,0,2:T(2,128)(2,1)}, u32[]{:S(2)}, u32[]{:S(2)}) %all-to-all-start) | async-done | bytes 4718624 | tf_op jit(solution)/shard_map/all_to_all | solution.py:44
  137.5 15.6 %gather_fusion.4 = bf16[128,2,12,768]{3,1,2,0:T(2,128)(2,1)} fusion(bf16[128,2,12,768]{3,1,2,0:T(2,128)(2,1)} %bitcast.8, s32[1024]{0:T(1024)S(1)} %pad_clamp_fusion), kind=kCustom, calls=%fused_computation.4 | custom fusion | bytes 9437696 | tf_op jit(solution)/shard_map/jit(_take)/gather | solution.py:45
  153.1 8.8 %fusion.6 = bf16[128,2,1,12,768]{4,1,3,2,0:T(2,128)(2,1)} fusion(bf16[128,2,12,768]{3,1,2,0:T(2,128)(2,1)} %gather_fusion.4, pred[128]{0:T(512)(128)(4,1)S(1)} %compare_and_fusion), kind=kLoop, calls=%fused_computation.13 | loop fusion | flops 2359296 | bytes 9437312 | tf_op jit(solution)/shard_map/jit(_take)/select_n | solution.py:45
  161.9 6.1 %all-to-all-start.1 = ((bf16[128,2,1,12,768]{4,1,3,2,0:T(2,128)(2,1)}), bf16[128,2,1,12,768]{4,1,3,2,0:T(2,128)(2,1)}, u32[]{:S(2)}, u32[]{:S(2)}) async-start(bf16[128,2,1,12,768]{4,1,3,2,0:T(2,128)(2,1)} %fusion.6), calls=%async_computation.1 | async-start | bytes 9437184 | tf_op jit(solution)/shard_map/all_to_all | solution.py:46
  168.1 0.0 copy-start.1
  168.1 1.6 fusion.33
  169.6 1.3 collective-permute-start
  170.9 1.4 collective-permute-start.1
  172.4 0.1 compare_select_fusion.7
  172.5 1.2 gather_fusion
  173.6 0.7 and_select_fusion.3
  174.3 0.1 broadcast_add_fusion
  174.4 0.7 add.175
  175.1 1.2 gather_fusion.1
  176.3 0.5 compare_and_fusion.1
  176.8 0.7 fusion.30
  177.5 0.7 and_select_fusion.1
  178.2 1.3 compare_and_fusion.2
  179.4 0.1 iota_compare_fusion
  179.5 18.7 %collective-permute-done = bf16[1,768,768]{2,1,0:T(8,128)(2,1)S(1)} collective-permute-done((bf16[1,768,768]{2,1,0:T(8,128)(2,1)}, bf16[1,768,768]{2,1,0:T(8,128)(2,1)S(1)}, u32[]{:S(2)}, u32[]{:S(2)}) %collective-permute-start) | collective-permute-done | bytes 1179680 | tf_op jit(solution)/shard_map/ppermute | solution.py:13
  198.2 0.0 collective-permute-done.1
  198.2 3.7 %maximum_select_fusion = bf16[4,768,768]{2,1,0:T(8,128)(2,1)} fusion(bf16[1,768,768]{2,1,0:T(8,128)(2,1)} %collective-permute-done.1, bf16[2,768,768]{2,1,0:T(8,128)(2,1)S(1)} %copy-done.2, bf16[1,768,768]{2,1,0:T(8,128)(2,1)S(1)} %collective-permute-done, pred[4,768]{1,0:T(4,128)(4,1)S(1)} %iota_compare_fusion), kind=kLoop, calls=%fused_computation.6 | loop fusion | flops 7077888 | bytes 9440256 | tf_op jit(solution)/shard_map/jit(_where)/select_n | solution.py:37
  201.9 5.3 %gather_fusion.2 = bf16[4,768,768]{2,1,0:T(8,128)(2,1)} fusion(bf16[4,768,768]{2,1,0:T(8,128)(2,1)} %maximum_select_fusion, s32[1024]{0:T(1024)S(1)} %pad_clamp_fusion.2), kind=kCustom, calls=%fused_computation.2 | custom fusion | bytes 9437200 | tf_op jit(solution)/shard_map/jit(_take)/gather | solution.py:52
  207.2 6.6 %copy.11 = bf16[2,2,768,768]{2,3,1,0:T(8,128)(2,1)} copy(bf16[2,2,768,768]{3,2,1,0:T(8,128)(2,1)} %bitcast.32) | data formatting | bytes 9437184 | tf_op jit(solution)/shard_map/jit(_take)/gather | solution.py:52
  213.8 3.0 %gather_fusion.3 = bf16[2,768,768]{2,1,0:T(8,128)(2,1)S(1)} fusion(bf16[4,768,768]{2,1,0:T(8,128)(2,1)} %maximum_select_fusion, s32[1024]{0:T(1024)S(1)} %pad_clamp_fusion.1), kind=kCustom, calls=%fused_computation.3 | custom fusion | bytes 4718600 | tf_op jit(solution)/shard_map/jit(_take)/gather | solution.py:38
  216.9 58.3 %all-to-all-done.1 = bf16[128,2,1,12,768]{4,1,3,2,0:T(2,128)(2,1)} async-done(((bf16[128,2,1,12,768]{4,1,3,2,0:T(2,128)(2,1)}), bf16[128,2,1,12,768]{4,1,3,2,0:T(2,128)(2,1)}, u32[]{:S(2)}, u32[]{:S(2)}) %all-to-all-start.1) | async-done | bytes 4718624 | tf_op jit(solution)/shard_map/all_to_all | solution.py:46
  275.2 7.8 %copy.15 = bf16[64,2,2,1,12,768]{5,2,4,0,1,3:T(2,128)(2,1)} copy(bf16[64,2,2,1,12,768]{5,2,4,1,0,3:T(2,128)(2,1)} %bitcast.11) | data formatting | bytes 9437184 | tf_op jit(solution)/shard_map/all_to_all | solution.py:46
  282.9 12.2 %fusion.8 = bf16[2,2,768,768]{3,2,1,0:T(8,128)(2,1)} fusion(bf16[2,2,768,768]{2,3,1,0:T(8,128)(2,1)} %copy.11, pred[2,2]{1,0:T(4,128)(4,1)S(1)} %copy-done.6, bf16[2,2,768,768]{3,1,2,0:T(2,128)(2,1)} %bitcast.34, bf16[2,768,768]{2,1,0:T(8,128)(2,1)S(1)} %gather_fusion.3, pred[2]{0:T(512)(128)(4,1)S(1)} %copy-done.7), kind=kOutput, calls=%fused_computation.15 | convolution fusion | flops 7256014848 | bytes 16515078 | tf_op jit(solution)/shard_map/psba,psbc->psac/dot_general | solution.py:54
  (25 shorter events, 0.1 us)
Async XLA Ops:
  0.0 175.1 %copy-start = (s32[8]{0:T(128)S(1)}, s32[8]{0:T(128)}, u32[]{:S(2)}) copy-start(s32[8]{0:T(128)} %param.9) | copy-start | bytes 100
  17.1 13.3 %copy-start.5 = (s32[128]{0:T(128)S(1)}, s32[128]{0:T(128)}, u32[]{:S(2)}) copy-start(s32[128]{0:T(128)} %param.8) | copy-start | bytes 1540
  17.1 120.4 %all-to-all-start = ((bf16[2,2,64,12,768]{4,1,3,0,2:T(2,128)(2,1)}), bf16[2,2,64,12,768]{4,1,3,0,2:T(2,128)(2,1)}, u32[]{:S(2)}, u32[]{:S(2)}) async-start(bf16[2,2,64,12,768]{4,1,3,0,2:T(2,128)(2,1)} %copy.13), calls=%async_computation | async-start | bytes 9437184 | tf_op jit(solution)/shard_map/all_to_all | solution.py:44
  33.0 139.4 %copy-start.4 = (s32[128]{0:T(128)}, s32[128]{0:T(128)S(1)}, u32[]{:S(2)}) copy-start(s32[128]{0:T(128)S(1)} %get-tuple-element.6) | copy-start | bytes 1540
  161.9 6.1 %copy-start.2 = (bf16[2,768,768]{2,1,0:T(8,128)(2,1)S(1)}, bf16[2,768,768]{2,1,0:T(8,128)(2,1)}, u32[]{:S(2)}) copy-start(bf16[2,768,768]{2,1,0:T(8,128)(2,1)} %param.6) | copy-start | bytes 7077892
  161.9 113.3 %all-to-all-start.1 = ((bf16[128,2,1,12,768]{4,1,3,2,0:T(2,128)(2,1)}), bf16[128,2,1,12,768]{4,1,3,2,0:T(2,128)(2,1)}, u32[]{:S(2)}, u32[]{:S(2)}) async-start(bf16[128,2,1,12,768]{4,1,3,2,0:T(2,128)(2,1)} %fusion.6), calls=%async_computation.1 | async-start | bytes 9437184 | tf_op jit(solution)/shard_map/all_to_all | solution.py:46
  168.1 4.4 %copy-start.1 = (s32[128]{0:T(128)S(1)}, s32[128]{0:T(128)}, u32[]{:S(2)}) copy-start(s32[128]{0:T(128)} %param.7) | copy-start | bytes 1540
  169.6 28.6 %collective-permute-start = (bf16[1,768,768]{2,1,0:T(8,128)(2,1)}, bf16[1,768,768]{2,1,0:T(8,128)(2,1)S(1)}, u32[]{:S(2)}, u32[]{:S(2)}) collective-permute-start(bf16[1,768,768]{2,1,0:T(8,128)(2,1)} %get-tuple-element.7), channel_id=1, source_target_pairs={{0,1},{1,2},{2,3},{3,0},{4,5},{5,6},{6,7},{7,4},{8,9},{9,10},{10,1... | collective-permute-start | bytes 3538952 | tf_op jit(solution)/shard_map/ppermute | solution.py:13
  170.9 27.3 %collective-permute-start.1 = (bf16[1,768,768]{2,1,0:T(8,128)(2,1)}, bf16[1,768,768]{2,1,0:T(8,128)(2,1)}, u32[]{:S(2)}, u32[]{:S(2)}) collective-permute-start(bf16[1,768,768]{2,1,0:T(8,128)(2,1)} %get-tuple-element.8), channel_id=1, source_target_pairs={{1,0},{2,1},{3,2},{0,3},{5,4},{6,5},{7,6},{4,7},{9,8},{10,9},{11,1... | collective-permute-start | bytes 3538952 | tf_op jit(solution)/shard_map/ppermute | solution.py:16
  174.3 3.2 %copy-start.3 = (s32[2]{0:T(128)}, s32[2]{0:T(128)S(1)}, u32[]{:S(2)}) copy-start(s32[2]{0:T(128)S(1)} %get-tuple-element.10) | copy-start | bytes 28
  275.2 7.8 %copy-start.6 = (pred[2,2]{1,0:T(4,128)(4,1)S(1)}, pred[2,2]{1,0:T(4,128)(4,1)}, u32[]{:S(2)}) copy-start(pred[2,2]{1,0:T(4,128)(4,1)} %compare_and_fusion.2) | copy-start | bytes 16
  275.2 7.8 %copy-start.7 = (pred[2]{0:T(512)(128)(4,1)S(1)}, pred[2]{0:T(512)(128)(4,1)}, u32[]{:S(2)}) copy-start(pred[2]{0:T(512)(128)(4,1)} %compare_and_fusion.1) | copy-start | bytes 10
where the time goes:
time: 296 us; the launch traced here: 295 us
  waiting for transfers between devices  181 us (61%)
  local copies, waits for them, and re-layouts  60.1 us (20%)
  starting transfers between devices  22.2 us (8%)
  other arithmetic  19.1 us (6%)
  matrix products  12.2 us (4%)
    all_to_all x1, waiting for transfers between devices, body(): lax.all_to_all(split, 'ops', split_axis=2, concat_axis=0, tiled=True)  105 us
    all_to_all x1, waiting for transfers between devices, body(): lax.all_to_all(ordered, 'ops', split_axis=0, concat_axis=2, tiled=True)  58.3 us
    ppermute x1, waiting for transfers between devices, with_halo(): lax.ppermute(lax.slice_in_dim(block, block.shape[dim] - width, None, axis...  18.7 us
    gather x1, local copies, waits for them, and re-layouts, body(): ordered = jnp.take(spread, source, axis=0)  15.6 us
    all_to_all x1, starting transfers between devices, body(): lax.all_to_all(split, 'ops', split_axis=2, concat_axis=0, tiled=True)  13.3 us
    dot_general x1, matrix products, body(): jnp.einsum('psba,psbc->psac', targets, half, preferred_element_type=jnp.f...  12.2 us
    gather x2, local copies, waits for them, and re-layouts, body(): targets = jnp.take(kept_near, target_local.reshape(-1), axis=0)  12 us
    unnamed x17, local copies, waits for them, and re-layouts  9.42 us
  transfers between devices with their start and end apart: 4, of which 3 were waited for; matrix products, arithmetic and copies ran while one was open for 10% of the time, Pallas kernels for 0%

commit v1 on v0

v1 whole, which is shorter than its diff:
```python
import functools

import jax
import jax.numpy as jnp
from jax import lax
from jax.experimental import pallas as pl
from jax.experimental.pallas import tpu as pltpu
from jax.sharding import PartitionSpec as P

HBM = pl.BlockSpec(memory_space=pl.ANY)
VMEM = pl.BlockSpec(memory_space=pltpu.VMEM)
SMEM = pl.BlockSpec(memory_space=pltpu.SMEM)
LANES = 128
SUBLANES = 8
STEP = 16
TILE = 256


def times_transposed(left, right):
    return lax.dot_general(
        left, right, (((1,), (1,)), ((), ())), preferred_element_type=jnp.float32
    )


def layout_of(sizes_ref, sectors):
    heights = [pl.cdiv(sizes_ref[sector], STEP) * STEP for sector in range(sectors)]
    starts = [0]
    for height in heights:
        starts.append(starts[-1] + height)
    return heights, starts


def halve_kernel(
    sizes_ref, operators_ref, basis_ref, out_ref,
    blocks, own, turned, half, packed, block_sem, own_sem, out_sem,
):
    pairs, sectors, width = blocks.shape[0], blocks.shape[1], blocks.shape[3]
    count, rows = out_ref.shape[0], out_ref.shape[2]
    heights, starts = layout_of(sizes_ref, sectors)

    def fetch_own(sector):
        return pltpu.make_async_copy(
            basis_ref.at[sector], own.at[sector], own_sem.at[sector]
        )

    def fetch(pair, sector):
        return pltpu.make_async_copy(
            operators_ref.at[pair, sector],
            blocks.at[pair, sector],
            block_sem.at[pair * sectors + sector],
        )

    for pair in range(pairs):
        for sector in range(sectors):
            if pair == 0:
                fetch_own(sector).start()
            fetch(pair, sector).start()

    for pair in range(pairs):
        for sector in range(sectors):
            if pair == 0:
                fetch_own(sector).wait()
                for tile in range(width // TILE):
                    span = slice(tile * TILE, (tile + 1) * TILE)
                    index = tile * TILE + lax.broadcasted_iota(jnp.int32, (TILE, width), 0)
                    strip = own[sector, :, span].T
                    turned[sector, span, :] = jnp.where(
                        index < sizes_ref[sector], strip, jnp.zeros_like(strip)
                    )
            fetch(pair, sector).wait()

            @pl.loop(0, width // TILE)
            def _(tile):
                span = pl.ds(pl.multiple_of(tile * TILE, TILE), TILE)
                half[span, :] = times_transposed(
                    turned[sector, span, :], blocks[pair, sector]
                ).astype(half.dtype)

            @pl.loop(0, heights[sector] // STEP)
            def _(step):
                row = pl.multiple_of(step * STEP, STEP)
                for lane in range(width // LANES):
                    start = pl.multiple_of(
                        lane * starts[-1] + starts[sector] + row, STEP
                    )
                    packed[pair, pl.ds(start, STEP), :] = half[
                        pl.ds(row, STEP), lane * LANES : (lane + 1) * LANES
                    ]

        @pl.loop(0, count)
        def _(part):
            pltpu.make_async_copy(
                packed.at[pair, pl.ds(pl.multiple_of(part * rows, SUBLANES), rows)],
                out_ref.at[part, pair],
                out_sem,
            ).start()

    pltpu.make_async_copy(out_ref, out_ref, out_sem).wait()


def halve(sizes, operators, basis, count, rows):
    pairs, sectors, height, width = operators.shape
    dtype = operators.dtype
    return pl.pallas_call(
        halve_kernel,
        out_shape=jax.ShapeDtypeStruct((count, pairs, rows, LANES), dtype),
        in_specs=[SMEM, HBM, HBM],
        out_specs=HBM,
        scratch_shapes=[
            pltpu.VMEM(operators.shape, dtype),
            pltpu.VMEM(basis.shape, dtype),
            pltpu.VMEM((sectors, width, height), dtype),
            pltpu.VMEM((width, height), dtype),
            pltpu.VMEM((pairs, count * rows, LANES), dtype),
            pltpu.SemaphoreType.DMA((pairs * sectors,)),
            pltpu.SemaphoreType.DMA((sectors,)),
            pltpu.SemaphoreType.DMA,
        ],
        cost_estimate=pl.CostEstimate(
            flops=2 * operators.size * width,
            bytes_accessed=4 * operators.size,
            transcendentals=0,
        ),
        name="halve",
    )(sizes, operators, basis)


def reorder_kernel(dest_ref, in_ref, out_ref, out_sem):
    @pl.loop(0, in_ref.shape[0])
    def _(pair):
        pltpu.make_async_copy(
            in_ref.at[pair], out_ref.at[dest_ref[pair]], out_sem
        ).start()

    pltpu.make_async_copy(out_ref, out_ref, out_sem).wait()


def reorder(blocks, dest):
    return pl.pallas_call(
        reorder_kernel,
        out_shape=jax.ShapeDtypeStruct(blocks.shape, blocks.dtype),
        in_specs=[SMEM, VMEM],
        out_specs=HBM,
        scratch_shapes=[pltpu.SemaphoreType.DMA],
        cost_estimate=pl.CostEstimate(
            flops=0, bytes_accessed=4 * blocks.size, transcendentals=0
        ),
        name="reorder",
    )(dest, blocks)


def finish_kernel(
    sizes_ref, offset_ref, strips_ref, turned_ref, out_ref,
    packed, target, half, result, in_sem, target_sem, out_sem,
):
    pairs, sectors, width = result.shape[0], result.shape[1], result.shape[3]
    count, rows = strips_ref.shape[0], strips_ref.shape[2]
    heights, starts = layout_of(sizes_ref, sectors)

    def fetch(pair, sector):
        slot = pair * sectors + sector
        return pltpu.make_async_copy(
            turned_ref.at[sector + 1 + offset_ref[pair]],
            target.at[slot],
            target_sem.at[slot],
        )

    for pair in range(pairs):

        @pl.loop(0, count)
        def _(part):
            pltpu.make_async_copy(
                strips_ref.at[part, pair],
                packed.at[pair, pl.ds(pl.multiple_of(part * rows, SUBLANES), rows)],
                in_sem.at[pair],
            ).start()

        for sector in range(sectors):
            fetch(pair, sector).start()

    for pair in range(pairs):
        pltpu.make_async_copy(packed.at[pair], packed.at[pair], in_sem.at[pair]).wait()
        for sector in range(sectors):

            @pl.loop(0, heights[sector] // STEP)
            def _(step):
                row = pl.multiple_of(step * STEP, STEP)
                for lane in range(width // LANES):
                    start = pl.multiple_of(
                        lane * starts[-1] + starts[sector] + row, STEP
                    )
                    half[pl.ds(row, STEP), lane * LANES : (lane + 1) * LANES] = packed[
                        pair, pl.ds(start, STEP), :
                    ]

            @pl.loop(heights[sector] // STEP, width // STEP)
            def _(step):
                row = pl.multiple_of(step * STEP, STEP)
                half[pl.ds(row, STEP), :] = jnp.zeros((STEP, width), half.dtype)

            fetch(pair, sector).wait()

            @pl.loop(0, width // TILE)
            def _(tile):
                span = pl.ds(pl.multiple_of(tile * TILE, TILE), TILE)
                result[pair, sector, span, :] = times_transposed(
                    target[pair * sectors + sector, span, :], half[...]
                ).astype(result.dtype)
                pltpu.make_async_copy(
                    result.at[pair, sector, span], out_ref.at[pair, sector, span], out_sem
                ).start()

    pltpu.make_async_copy(out_ref, out_ref, out_sem).wait()


def finish(sizes, offsets, strips, turned, shape):
    pairs, sectors, height, width = shape
    count, _, rows, _ = strips.shape
    dtype = strips.dtype
    size = pairs * sectors * height * width
    return pl.pallas_call(
        finish_kernel,
        out_shape=jax.ShapeDtypeStruct(shape, dtype),
        in_specs=[SMEM, SMEM, VMEM, HBM],
        out_specs=HBM,
        scratch_shapes=[
            pltpu.VMEM((pairs, count * rows, LANES), dtype),
            pltpu.VMEM((pairs * sectors, height, width), dtype),
            pltpu.VMEM((width, height), dtype),
            pltpu.VMEM(shape, dtype),
            pltpu.SemaphoreType.DMA((pairs,)),
            pltpu.SemaphoreType.DMA((pairs * sectors,)),
            pltpu.SemaphoreType.DMA,
        ],
        cost_estimate=pl.CostEstimate(
            flops=2 * size * width, bytes_accessed=6 * size, transcendentals=0
        ),
        name="finish",
    )(sizes, offsets, strips, turned)


def body(operators, basis, shift, dest, sector_sizes):
    pairs, sectors, width = operators.shape[0], operators.shape[1], operators.shape[3]
    count = lax.axis_size("ops")
    sec_count = lax.axis_size("sec")
    total = sectors * sec_count
    sec_pos, ops_pos = lax.axis_index("sec"), lax.axis_index("ops")
    rows = sectors * width * width // (LANES * count)

    own_sizes = lax.dynamic_slice_in_dim(sector_sizes, sec_pos * sectors, sectors)
    strips = halve(own_sizes, operators, basis, count, rows)
    spread = lax.all_to_all(strips, "ops", 0, 0, tiled=True)

    forward = [(i, (i + 1) % sec_count) for i in range(sec_count)]
    backward = [(j, i) for i, j in forward]
    low = lax.ppermute(basis[-1:], "sec", forward)
    high = lax.ppermute(basis[:1], "sec", backward)
    near = jnp.concatenate([low, basis, high], axis=0)
    near_ids = (sec_pos * sectors - 1 + jnp.arange(sectors + 2, dtype=jnp.int32)) % total
    sizes = jnp.sum(
        jnp.where(
            near_ids[:, None] == jnp.arange(total, dtype=jnp.int32)[None, :],
            sector_sizes[None, :],
            0,
        ),
        axis=1,
    )
    kept = jnp.arange(width, dtype=jnp.int32)[None, :] < sizes[:, None]
    turned = jnp.swapaxes(jnp.where(kept[:, None, :], near, jnp.zeros_like(near)), 1, 2)
    mine = ops_pos * pairs + jnp.arange(pairs, dtype=jnp.int32)
    offsets = jnp.sum(jnp.where(mine[:, None] == dest[None, :], shift[None, :], 0), axis=1)

    ordered = reorder(spread.reshape((count * pairs,) + spread.shape[2:]), dest)
    back = lax.all_to_all(ordered.reshape(spread.shape), "ops", 0, 0, tiled=True)
    return finish(own_sizes, offsets, back, turned, operators.shape)


def solution(mesh):
    return jax.shard_map(
        body,
        mesh=mesh,
        in_specs=(P("ops", "sec", None, None), P("sec", None, None), P(), P(), P()),
        out_specs=P("ops", "sec", None, None),
        check_vma=False,
    )
```

time: 296 us -> 272 us (0.919)
  blocking collectives: 0 us -> 120 us
  waiting for transfers between devices: 181 us -> 95 us
  local copies, waits for them, and re-layouts: 60.1 us -> 5.7 us
  Pallas kernels: 0 us -> 36.3 us
  other arithmetic: 19.1 us -> 4.91 us
  starting transfers between devices: 22.2 us -> 9.14 us
  matrix products: 12.2 us -> 0 us
    all_to_all x0 -> x1, blocking collectives: none -> 120 us  [body(): spread = lax.all_to_all(strips, 'ops', 0, 0, tiled=True)]
    all_to_all x2 -> x1, waiting for transfers between devices: 163 us -> 70.1 us  [body(): lax.all_to_all(ordered.reshape(spread.shape), 'ops', 0, 0, tiled=True)]
    pallas_call x0 -> x3, Pallas kernels: none -> 36.3 us  [the longest x1 18.6 us: finish(): pl.pallas_call(finish_kernel, out_shape=jax.ShapeDtypeStruct(shape, dtype...]
    gather x6 -> x0, local copies, waits for them, and re-layouts: 32.9 us -> none  [the longest x1 15.6 us: body(): ordered = jnp.take(spread, source, axis=0)]
    select_n x9 -> x1, other arithmetic: 14.6 us -> 0.01 us  [body(): (sec_pos * sectors - 1 + jnp.arange(sectors + 2, dtype=jnp.int32)) % total]
    all_to_all x2 -> x1, starting transfers between devices: 19.4 us -> 6.46 us  [body(): lax.all_to_all(ordered.reshape(spread.shape), 'ops', 0, 0, tiled=True)]
    dot_general x1 -> x0, matrix products: 12.2 us -> none  [body(): jnp.einsum('psba,psbc->psac', targets, half, preferred_element_type=jnp.f...]
    all_to_all x1 -> x0, local copies, waits for them, and re-layouts: 7.75 us -> none  [body(): lax.all_to_all(ordered, 'ops', split_axis=0, concat_axis=2, tiled=True)]
  transfers between devices with their start and end apart: 4 -> 3, of which waited for: 3 -> 2; matrix products, arithmetic and copies ran while one was open for 10% -> 3% of each run, Pallas kernels for 0% -> 0%
where the time goes in v1:
time: 272 us; the launch traced here: 271 us
  blocking collectives  120 us (44%)
  waiting for transfers between devices  95 us (35%)
  Pallas kernels  36.3 us (13%)
  starting transfers between devices  9.14 us (3%)
  local copies, waits for them, and re-layouts  5.7 us (2%)
  other arithmetic  4.91 us (2%)
    all_to_all x1, blocking collectives, body(): spread = lax.all_to_all(strips, 'ops', 0, 0, tiled=True)  120 us
    all_to_all x1, waiting for transfers between devices, body(): lax.all_to_all(ordered.reshape(spread.shape), 'ops', 0, 0, tiled=True)  70.1 us
    ppermute x1, waiting for transfers between devices, body(): low = lax.ppermute(basis[-1:], 'sec', forward)  24.9 us
    pallas_call x1, Pallas kernels, finish(): pl.pallas_call(finish_kernel, out_shape=jax.ShapeDtypeStruct(shape, dtype...  18.6 us
    pallas_call x1, Pallas kernels, halve(): pl.pallas_call(halve_kernel, out_shape=jax.ShapeDtypeStruct((count, pairs...  13.2 us
    all_to_all x1, starting transfers between devices, body(): lax.all_to_all(ordered.reshape(spread.shape), 'ops', 0, 0, tiled=True)  6.46 us
  transfers between devices with their start and end apart: 3, of which 2 were waited for; matrix products, arithmetic and copies ran while one was open for 3% of the time, Pallas kernels for 0%

profile of v1, /device:TPU:1, one launch (start us, length us, event | category | flops | bytes accessed | tf_op | source)
XLA Modules:
  0.0 271.4 jit_solution(14951777229109506718)
XLA Ops:
  0.0 1.2 dynamic_slice.3.sizes_ref
  1.2 13.2 %halve.1 = bf16[64,2,144,128]{3,2,1,0:T(8,128)(2,1)} custom-call(s32[2]{0:T(128)} %dynamic_slice.3.sizes_ref, bf16[2,2,768,768]{3,2,1,0:T(8,128)(2,1)} %operators_ref.1, bf16[2,768,768]{2,1,0:T(8,128)(2,1)} %basis_ref.1), custom_call_target="tpu_custom_call" | custom-call | flops 3623878656 | bytes 9437184 | tf_op jit(solution)/shard_map/halve/pallas_call | solution.py:104
  14.5 120.3 %all_to_all.10 = bf16[64,2,144,128]{3,2,1,0:T(8,128)(2,1)} all-to-all(bf16[64,2,144,128]{3,2,1,0:T(8,128)(2,1)} %halve.1), channel_id=1, replica_groups=mesh['ops'=64,'sec'=4] {'ops'}, dimensions={0} | all-to-all | bytes 9437184 | tf_op jit(solution)/shard_map/all_to_all | solution.py:252
  134.8 4.5 %reorder.1 = bf16[128,144,128]{2,1,0:T(8,128)(2,1)} custom-call(s32[128]{0:T(128)} %dest_ref.1, bf16[128,144,128]{2,1,0:T(8,128)(2,1)} %bitcast.5), custom_call_target="tpu_custom_call" | custom-call | bytes 9437184 | tf_op jit(solution)/shard_map/reorder/pallas_call | solution.py:139
  139.3 6.5 %all-to-all-start.1 = ((bf16[64,2,144,128]{3,2,1,0:T(8,128)(2,1)}), bf16[64,2,144,128]{3,2,1,0:T(8,128)(2,1)}, u32[]{:S(2)}, u32[]{:S(2)}) async-start(bf16[64,2,144,128]{3,2,1,0:T(8,128)(2,1)} %bitcast.4), calls=%async_computation.1 | async-start | bytes 9437184 | tf_op jit(solution)/shard_map/all_to_all | solution.py:274
  145.7 0.0 copy-start.2
  145.7 0.0 copy-start
  145.8 0.0 copy-start.1
  145.8 2.8 %copy.9 = bf16[2,768,768]{1,2,0:T(8,128)(2,1)S(1)} copy(bf16[2,768,768]{2,1,0:T(8,128)(2,1)} %basis_ref.1) | data formatting | bytes 4718592 | tf_op args[1]
  148.6 1.6 fusion.3
  150.2 1.5 collective-permute-start
  151.7 1.2 collective-permute-start.1
  152.9 0.0 copy-done.2
  152.9 0.2 select_reduce_fusion
  153.1 0.0 copy-done
  153.1 0.0 copy-done.1
  153.1 0.7 fusion.1.offset_ref
  153.8 0.1 iota_compare_fusion
  153.8 24.9 %collective-permute-done = bf16[1,768,768]{1,2,0:T(8,128)(2,1)S(1)} collective-permute-done((bf16[1,768,768]{1,2,0:T(8,128)(2,1)}, bf16[1,768,768]{1,2,0:T(8,128)(2,1)S(1)}, u32[]{:S(2)}, u32[]{:S(2)}) %collective-permute-start) | collective-permute-done | bytes 1179680 | tf_op jit(solution)/shard_map/ppermute | solution.py:256
  178.7 0.0 collective-permute-done.1
  178.8 4.0 %fusion.turned_ref = bf16[4,768,768]{2,1,0:T(8,128)(2,1)} fusion(bf16[1,768,768]{1,2,0:T(8,128)(2,1)} %collective-permute-done.1, bf16[2,768,768]{1,2,0:T(8,128)(2,1)S(1)} %copy.9, bf16[1,768,768]{1,2,0:T(8,128)(2,1)S(1)} %collective-permute-done, pred[4,768]{1,0:T(4,128)(4,1)S(1)} %iota_compare_fusion), kind=kLoop, calls=%fused_computation.1 | loop fusion | flops 7077888 | bytes 9440256 | tf_op jit(solution)/shard_map/transpose | solution.py:269
  182.7 70.1 %all-to-all-done.1.strips_ref = bf16[64,2,144,128]{3,2,1,0:T(8,128)(2,1)} async-done(((bf16[64,2,144,128]{3,2,1,0:T(8,128)(2,1)}), bf16[64,2,144,128]{3,2,1,0:T(8,128)(2,1)}, u32[]{:S(2)}, u32[]{:S(2)}) %all-to-all-start.1) | async-done | bytes 4718624 | tf_op jit(solution)/shard_map/all_to_all | solution.py:274
  252.8 18.6 %finish.1 = bf16[2,2,768,768]{3,2,1,0:T(8,128)(2,1)} custom-call(s32[2]{0:T(128)} %dynamic_slice.3.sizes_ref, s32[2]{0:T(128)} %fusion.1.offset_ref, bf16[64,2,144,128]{3,2,1,0:T(8,128)(2,1)} %all-to-all-done.1.strips_ref, bf16[4,768,768]{2,1,0:T(8,128)(2,1)} %fusion.turned_ref), custom_call_target="tpu_custom_call" | custom-call | flops 3623878656 | bytes 14155776 | tf_op jit(solution)/shard_map/finish/pallas_call | solution.py:221
  (2 shorter events, 0.0 us)
Async XLA Ops:
  139.3 113.6 %all-to-all-start.1 = ((bf16[64,2,144,128]{3,2,1,0:T(8,128)(2,1)}), bf16[64,2,144,128]{3,2,1,0:T(8,128)(2,1)}, u32[]{:S(2)}, u32[]{:S(2)}) async-start(bf16[64,2,144,128]{3,2,1,0:T(8,128)(2,1)} %bitcast.4), calls=%async_computation.1 | async-start | bytes 9437184 | tf_op jit(solution)/shard_map/all_to_all | solution.py:274
  145.7 7.2 %copy-start.2 = (s32[8]{0:T(128)S(1)}, s32[8]{0:T(128)}, u32[]{:S(2)}) copy-start(s32[8]{0:T(128)} %param.9) | copy-start | bytes 100
  145.7 7.4 %copy-start = (s32[128]{0:T(128)S(1)}, s32[128]{0:T(128)}, u32[]{:S(2)}) copy-start(s32[128]{0:T(128)} %dest_ref.1) | copy-start | bytes 1540
  145.8 7.3 %copy-start.1 = (s32[128]{0:T(128)S(1)}, s32[128]{0:T(128)}, u32[]{:S(2)}) copy-start(s32[128]{0:T(128)} %param.7) | copy-start | bytes 1540
  150.2 28.5 %collective-permute-start = (bf16[1,768,768]{1,2,0:T(8,128)(2,1)}, bf16[1,768,768]{1,2,0:T(8,128)(2,1)S(1)}, u32[]{:S(2)}, u32[]{:S(2)}) collective-permute-start(bf16[1,768,768]{1,2,0:T(8,128)(2,1)} %get-tuple-element.5), channel_id=1, source_target_pairs={{0,1},{1,2},{2,3},{3,0},{4,5},{5,6},{6,7},{7,4},{8,9},{9,10},{10,1... | collective-permute-start | bytes 3538952 | tf_op jit(solution)/shard_map/ppermute | solution.py:256
  151.7 27.1 %collective-permute-start.1 = (bf16[1,768,768]{1,2,0:T(8,128)(2,1)}, bf16[1,768,768]{1,2,0:T(8,128)(2,1)}, u32[]{:S(2)}, u32[]{:S(2)}) collective-permute-start(bf16[1,768,768]{1,2,0:T(8,128)(2,1)} %get-tuple-element.6), channel_id=1, source_target_pairs={{1,0},{2,1},{3,2},{0,3},{5,4},{6,5},{7,6},{4,7},{9,8},{10,9},{11,1... | collective-permute-start | bytes 3538952 | tf_op jit(solution)/shard_map/ppermute | solution.py:257
